TPU v7x, 32 devices: a whole 2x2x4 slice. The times are simulated.
32 devices in a mesh: outer: 4 (over y, x), inner: 8 (over z, core).
Axes of the slice: x: 2, y: 2, z: 4, core: 2. Of those that a mesh axis runs over, the one named last changes fastest.
Arguments:
- acts: bfloat16 [32, 2, 512, 512], P(('outer', 'inner')), may hold values from -6 to 6
- cotangent: bfloat16 [32, 2, 512, 512], P(('outer', 'inner')), may hold values from -6 to 6
- residual: float32 [32, 2048, 128], P(('outer', 'inner')), may hold values from -0.6 to 0.6
- owner_residual: float32 [32, 256, 128], P(('outer', 'inner')), may hold values from -3 to 3
- in_count: int32 [32, 2, 8], P(('outer', 'inner')), may hold values from 1 to 128, as said below
- in_rank: int32 [32, 2, 2048], P(('outer', 'inner')), may hold values from 0 to 255, as said below
- out_count: int32 [32, 2], P(('outer', 'inner')), may hold values from 1 to 128
- out_rank: int32 [32, 2, 256], P(('outer', 'inner')), may hold values from 0 to 255, as said below
Outputs:
- applied: bfloat16 [512, 512], replicated
- new_residual: float32 [32, 2048, 128], P(('outer', 'inner'))
- new_owner_residual: float32 [32, 256, 128], P(('outer', 'inner'))
Inputs may be any that keep to these rules, and one draw needn't show every extreme that they name: `in_count`: each step has one owner that receives 128 blocks from every replica. `in_rank`: for each replica, step and owner, the ranks of that owner's 256 blocks are a permutation of 0 to 255. `out_rank`: for each replica and step a permutation of 0 to 255.
All inputs are finite; a program needn't handle non-finite values.
Results may differ from a plain program's by a relative error of at most 0.0065.
Values may be sent and summed in bfloat16 or wider, within the bound.
A program may use at most 64 MiB of HBM per device.

v0:
```python
import math

import jax
import jax.numpy as jnp
from jax import lax
from jax.sharding import PartitionSpec as P

step_size = 0.0625


def select_blocks(resid, grad, ranks_flat, counts, owners, region, width):
    blocks = resid.shape[0]
    accum = (resid + grad.reshape(blocks, width)).reshape(owners, region, width)
    ranks = ranks_flat.reshape(owners, region)
    chosen = (ranks < counts[:, None])[..., None]
    new_resid = jnp.where(chosen, jnp.float32(0.0), accum).reshape(blocks, width)
    return (accum, ranks, chosen, new_resid)


def pack_slots(accum, ranks, counts, slots, region):
    order = lax.iota(jnp.int32, slots)
    picks = (ranks[:, None, :] == order[None, :, None]) & (
        order[None, :, None] < counts[:, None, None]
    )
    picks_f = picks.astype(jnp.float32)
    places = lax.iota(jnp.int32, region).astype(jnp.float32)
    packed = jnp.einsum("nkr,nrd->nkd", picks_f, accum, precision=lax.Precision.HIGHEST)
    where_at = jnp.einsum("nkr,r->nk", picks_f, places, precision=lax.Precision.HIGHEST)
    return (packed, where_at)


def unpack_slots(arrived, spots, region, width):
    places = lax.iota(jnp.int32, region).astype(jnp.float32)
    placed = (spots.reshape(-1)[:, None] == places[None, :]).astype(jnp.float32)
    return jnp.einsum(
        "mr,md->rd", placed, arrived.reshape(-1, width), precision=lax.Precision.HIGHEST
    )


def owner_section(pod_sum, oresid, ranks_out, count_out):
    owner_acc = pod_sum + oresid
    passed = (ranks_out < count_out)[:, None]
    outgoing = jnp.where(passed, owner_acc, jnp.float32(0.0))
    kept = jnp.where(passed, jnp.float32(0.0), owner_acc)
    return (outgoing, kept)


def per_device(acts, cotangent, residual, owner_residual, in_count, in_rank, out_count, out_rank):
    owners = lax.axis_size("inner")
    steps = acts.shape[1]
    tokens = acts.shape[2]
    rows = acts.shape[3]
    cols = cotangent.shape[3]
    blocks = residual.shape[1]
    width = residual.shape[2]
    region = blocks // owners
    slots = max(1, region // 2)
    scale = 1.0 / math.sqrt(tokens * owners)
    resid = residual[0]
    oresid = owner_residual[0]
    crosses = []
    packs = []
    spots_all = []
    for step in range(steps):
        grad = (
            jnp.einsum(
                "tr,tc->rc", acts[0, step], cotangent[0, step], preferred_element_type=jnp.float32
            )
            * scale
        )
        counts = in_count[0, step]
        accum, ranks, chosen, resid = select_blocks(
            resid, grad, in_rank[0, step], counts, owners, region, width
        )
        packed, where_at = pack_slots(accum, ranks, counts, slots, region)
        packs.append(packed)
        spots_all.append(where_at)
    arrived, spots = (
        lax.all_to_all(
            jnp.concatenate(packs, axis=1), "inner", split_axis=0, concat_axis=0, tiled=True
        ),
        lax.all_to_all(
            jnp.concatenate(spots_all, axis=1), "inner", split_axis=0, concat_axis=0, tiled=True
        ),
    )
    outgoings = []
    for step in range(steps):
        pod_sum = unpack_slots(
            arrived[:, step * slots : (step + 1) * slots],
            spots[:, step * slots : (step + 1) * slots],
            region,
            width,
        )
        outgoing, oresid = owner_section(pod_sum, oresid, out_rank[0, step], out_count[0, step])
        outgoings.append(outgoing)
    summed = lax.psum(jnp.stack(outgoings), "outer")
    for step in range(steps):
        crosses.append(summed[step])
    deltas = []
    for cross in crosses:
        delta = cross.astype(jnp.bfloat16)
        deltas.append(lax.all_gather(delta, "inner", axis=0, tiled=True))
    total = deltas[0].astype(jnp.float32)
    for later in deltas[1:]:
        total = total + later.astype(jnp.float32)
    applied = (-step_size * total).astype(jnp.bfloat16)
    return (applied.reshape(rows, cols), resid[None], oresid[None])


def solution(mesh):
    return jax.shard_map(
        per_device,
        mesh=mesh,
        in_specs=(
            P(("outer", "inner"), None, None, None),
            P(("outer", "inner"), None, None, None),
            P(("outer", "inner"), None, None),
            P(("outer", "inner"), None, None),
            P(("outer", "inner"), None, None),
            P(("outer", "inner"), None, None),
            P(("outer", "inner"), None),
            P(("outer", "inner"), None, None),
        ),
        out_specs=(P(), P(("outer", "inner"), None, None), P(("outer", "inner"), None, None)),
        check_vma=False,
    )
```

profile of v0, /device:TPU:1, one launch (start us, length us, event | category | flops | bytes accessed | tf_op | source)
XLA Modules:
  0.0 107.3 jit_solution(2119383466452367216)
XLA Ops:
  0.7 0.6 copy-done.8
  1.3 0.8 slice_reduce_fusion.1
  2.9 0.6 fusion.10
  4.1 6.4 %all-to-all-start = ((f32[8,1,256]{2,1,0:T(1,128)}), f32[8,1,256]{2,1,0:T(1,128)S(1)}, u32[]{:S(2)}, u32[]{:S(2)}) async-start(f32[8,1,256]{2,1,0:T(1,128)} %all_to_all.11), calls=%async_computation | async-start | bytes 16384 | tf_op jit(solution)/shard_map/all_to_all | solution.py:82
  10.6 1.6 %convolution_multiply_fusion = f32[512,512]{1,0:T(8,128)S(1)} fusion(bf16[1,2,512,512]{3,2,1,0:T(8,128)(2,1)S(1)} %copy-done.9, bf16[1,2,512,512]{3,2,1,0:T(8,128)(2,1)} %param.8), kind=kOutput, calls=%fused_computation | convolution fusion | flops 268697600 | bytes 2097152 | tf_op jit(solution)/shard_map/tr,tc->rc/dot_general | solution.py:66
  12.7 1.0 copy-done.2
  13.8 1.0 reshape.168
  15.4 0.9 fusion.4
  16.6 1.6 %fusion = f32[8,128,128]{2,1,0:T(8,128)S(1)} fusion(f32[8,256,128]{2,1,0:T(8,128)S(1)} %copy-done.4, s32[8,256]{1,0:T(8,128)S(1)} %eq.64, pred[8,256]{1,0:T(8,128)(4,1)S(1)} %broadcast_compare_fusion, pred[8,128]{1,0:T(8,128)(4,1)S(1)} %get-tuple-element.23, f32[8,256,128]{2,1,0:T(8,128)S(1)} %bitcast.55, f32[8,256,128]{2,1,0:T(8,128)S(1)} %reshape.167), kind=kOutput, calls=%fused_computation.7 | convolution fusion | flops 403963904 | bytes 3681280 | tf_op jit(solution)/shard_map/nkr,nrd->nkd/dot_general | solution.py:27
  18.2 1.1 pad_maximum_fusion
  19.3 5.2 %all-to-all-start.1 = ((f32[8,256,128]{2,1,0:T(8,128)}), f32[8,256,128]{2,1,0:T(8,128)}, u32[]{:S(2)}, u32[]{:S(2)}) async-start(f32[8,256,128]{2,1,0:T(8,128)} %pad_maximum_fusion), calls=%async_computation.1 | async-start | bytes 2097152 | tf_op jit(solution)/shard_map/all_to_all | solution.py:79
  24.6 1.3 %reshape.173 = f32[1,2048,128]{2,1,0:T(8,128)S(1)} reshape(f32[512,512]{1,0:T(8,128)} %copy-done.1) | data formatting | bytes 2097152 | tf_op jit(solution)/shard_map/reshape | solution.py:13
  26.0 0.6 copy-done.7
  27.2 0.7 copy-done.6
  27.9 1.3 %compare_reduce_fusion = (pred[256]{0:T(512)(128)(4,1)S(1)}, pred[256]{0:T(512)(128)(4,1)S(1)}) fusion(s32[1,2,256]{2,1,0:T(2,128)S(1)} %copy-done.6, s32[]{:T(128)} %bitcast.18, s32[]{:T(128)} %bitcast), kind=kLoop, calls=%fused_computation.56 | loop fusion | flops 512 | bytes 2568 | tf_op jit(solution)/shard_map/lt | solution.py:42
  29.2 2.4 %add_select_fusion = f32[1,2048,128]{2,1,0:T(8,128)} fusion(f32[1,2048,128]{2,1,0:T(8,128)S(1)} %reshape.173, f32[1,2048,128]{2,1,0:T(8,128)S(1)} %copy-done, f32[1,2048,128]{2,1,0:T(8,128)S(1)} %reshape.172, pred[2048]{0:T(1024)(128)(4,1)S(1)} %lt.117, pred[2048]{0:T(1024)(128)(4,1)S(1)} %lt.115), kind=kLoop, calls=%fused_computation.6 | loop fusion | flops 1048576 | bytes 4198400 | tf_op jit(solution)/shard_map/jit(_where)/select_n | solution.py:16
  31.7 18.6 %all-to-all-done.1 = f32[8,256,128]{2,1,0:T(8,128)} async-done(((f32[8,256,128]{2,1,0:T(8,128)}), f32[8,256,128]{2,1,0:T(8,128)}, u32[]{:S(2)}, u32[]{:S(2)}) %all-to-all-start.1) | async-done | bytes 1048608 | tf_op jit(solution)/shard_map/all_to_all | solution.py:79
  50.2 1.3 %fusion.39 = (f32[8,128,128]{2,1,0:T(8,128)S(1)}, f32[8,128,128]{2,1,0:T(8,128)S(1)}) fusion(f32[8,256,128]{2,1,0:T(8,128)} %all-to-all-done.1), kind=kLoop, calls=%fused_computation.64 | loop fusion | bytes 2097152 | tf_op jit(solution)/shard_map/slice | solution.py:89
  51.5 1.2 %convolution_add_fusion.1 = f32[256,128]{1,0:T(8,128)S(1)} fusion(f32[1024,128]{1,0:T(8,128)S(1)} %bitcast.57, f32[256]{0:T(256)S(1)} %iota_convert_fusion, f32[1024]{0:T(1024)S(1)} %get-tuple-element.15, f32[1,256,128]{2,1,0:T(8,128)S(1)} %copy-done.5), kind=kOutput, calls=%fused_computation.3 | convolution fusion | flops 402948096 | bytes 791552 | tf_op jit(solution)/shard_map/mr,md->rd/dot_general | solution.py:35
  52.8 1.8 %select_bitcast_fusion = (f32[1,256,128]{2,1,0:T(8,128)}, f32[1,256,128]{2,1,0:T(8,128)S(1)}) fusion(pred[256]{0:T(512)(128)(4,1)S(1)} %get-tuple-element.5, f32[256,128]{1,0:T(8,128)S(1)} %convolution_add_fusion.1, pred[256]{0:T(512)(128)(4,1)S(1)} %get-tuple-element.6, f32[1024,128]{1,0:T(8,128)S(1)} %bitcast.56, f32[256]{0:T(256)S(1)} %iota_convert_fusion, ...), kind=kOutput, calls=%fused_computation.44 | convolution fusion | flops 403046400 | bytes 923136 | tf_op jit(solution)/shard_map/mr,md->rd/dot_general | solution.py:35
  54.6 16.5 %all-reduce.1 = bf16[2,256,128]{2,1,0:T(8,128)(2,1)S(1)} all-reduce(f32[2,256,128]{2,1,0:T(8,128)S(1)} %pad_maximum_fusion.1), channel_id=1, replica_groups=mesh['outer'=4,'inner'=8] {'outer'}, use_global_device_ids=true, to_apply=%region_0.1 | all-reduce | flops 65536 | bytes 393216 | tf_op jit(solution)/shard_map/psum | solution.py:96
  71.2 20.1 %all-gather = bf16[1,2048,128]{2,1,0:T(8,128)(2,1)S(1)} all-gather(bf16[1,256,128]{2,1,0:T(8,128)(2,1)S(1)} %get-tuple-element.11), channel_id=2, replica_groups=mesh['outer'=4,'inner'=8] {'inner'}, dimensions={1}, use_global_device_ids=true | all-gather | bytes 589824 | tf_op jit(solution)/shard_map/all_gather | solution.py:102
  91.2 14.8 %all-gather.1 = bf16[1,2048,128]{2,1,0:T(8,128)(2,1)S(1)} all-gather(bf16[1,256,128]{2,1,0:T(8,128)(2,1)S(1)} %get-tuple-element.12), channel_id=3, replica_groups=mesh['outer'=4,'inner'=8] {'inner'}, dimensions={1}, use_global_device_ids=true | all-gather | bytes 589824 | tf_op jit(solution)/shard_map/all_gather | solution.py:102
  106.2 1.1 %reshape.171 = bf16[512,512]{1,0:T(8,128)(2,1)} reshape(bf16[1,2048,128]{2,1,0:T(8,128)(2,1)S(1)} %multiply_convert_fusion) | data formatting | bytes 1048576 | tf_op jit(solution)/shard_map/reshape | solution.py:107
  (43 shorter events, 3.9 us)
Async XLA Ops:
  0.6 0.7 copy-start.8
  0.6 9.9 %copy-start.9 = (bf16[1,2,512,512]{3,2,1,0:T(8,128)(2,1)S(1)}, bf16[1,2,512,512]{3,2,1,0:T(8,128)(2,1)}, u32[]{:S(2)}) copy-start(bf16[1,2,512,512]{3,2,1,0:T(8,128)(2,1)} %param.9) | copy-start | bytes 3145732
  4.1 15.2 %all-to-all-start = ((f32[8,1,256]{2,1,0:T(1,128)}), f32[8,1,256]{2,1,0:T(1,128)S(1)}, u32[]{:S(2)}, u32[]{:S(2)}) async-start(f32[8,1,256]{2,1,0:T(1,128)} %all_to_all.11), calls=%async_computation | async-start | bytes 16384 | tf_op jit(solution)/shard_map/all_to_all | solution.py:82
  10.6 1.6 %copy-start.10 = (bf16[1,2,512,512]{3,2,1,0:T(8,128)(2,1)S(1)}, bf16[1,2,512,512]{3,2,1,0:T(8,128)(2,1)}, u32[]{:S(2)}) copy-start(bf16[1,2,512,512]{3,2,1,0:T(8,128)(2,1)} %param.8) | copy-start | bytes 3145732
  12.2 1.6 %copy-start.1 = (f32[512,512]{1,0:T(8,128)}, f32[512,512]{1,0:T(8,128)S(1)}, u32[]{:S(2)}) copy-start(f32[512,512]{1,0:T(8,128)S(1)} %convolution_multiply_fusion) | copy-start | bytes 3145732
  12.7 1.0 copy-start.2
  13.8 1.6 %copy-start = (f32[1,2048,128]{2,1,0:T(8,128)S(1)}, f32[1,2048,128]{2,1,0:T(8,128)}, u32[]{:S(2)}) copy-start(f32[1,2048,128]{2,1,0:T(8,128)} %param.10) | copy-start | bytes 3145732
  15.4 1.2 %copy-start.4 = (f32[8,256,128]{2,1,0:T(8,128)S(1)}, f32[8,256,128]{2,1,0:T(8,128)}, u32[]{:S(2)}) copy-start(f32[8,256,128]{2,1,0:T(8,128)} %reshape.168) | copy-start | bytes 3145732
  19.3 5.2 %copy-start.3 = (f32[512,512]{1,0:T(8,128)S(1)}, f32[512,512]{1,0:T(8,128)}, u32[]{:S(2)}) copy-start(f32[512,512]{1,0:T(8,128)} %copy-done.2) | copy-start | bytes 3145732
  19.3 30.9 %all-to-all-start.1 = ((f32[8,256,128]{2,1,0:T(8,128)}), f32[8,256,128]{2,1,0:T(8,128)}, u32[]{:S(2)}, u32[]{:S(2)}) async-start(f32[8,256,128]{2,1,0:T(8,128)} %pad_maximum_fusion), calls=%async_computation.1 | async-start | bytes 2097152 | tf_op jit(solution)/shard_map/all_to_all | solution.py:79
  26.0 0.7 copy-start.7
  27.2 0.7 copy-start.6
  31.7 19.9 %copy-start.5 = (f32[1,256,128]{2,1,0:T(8,128)S(1)}, f32[1,256,128]{2,1,0:T(8,128)}, u32[]{:S(2)}) copy-start(f32[1,256,128]{2,1,0:T(8,128)} %param.11) | copy-start | bytes 393220
where the time goes:
time: 108 us; the launch traced here: 107 us
  blocking collectives  51.4 us (48%)
  waiting for transfers between devices  18.6 us (17%)
  starting transfers between devices  11.6 us (11%)
  local copies, waits for them, and re-layouts  10.9 us (10%)
  matrix products  8.8 us (8%)
  other arithmetic  5.26 us (5%)
    all_gather x2, blocking collectives, per_device(): deltas.append(lax.all_gather(delta, 'inner', axis=0, tiled=True))  34.8 us
    all_to_all x1, waiting for transfers between devices, per_device(): lax.all_to_all(jnp.concatenate(packs, axis=1), 'inner', split_axis=0, con...  18.6 us
    psum x1, blocking collectives, per_device(): summed = lax.psum(jnp.stack(outgoings), 'outer')  16.5 us
    all_to_all x1, starting transfers between devices, per_device(): lax.all_to_all(jnp.concatenate(spots_all, axis=1), 'inner', split_axis=0,...  6.37 us
    all_to_all x1, starting transfers between devices, per_device(): lax.all_to_all(jnp.concatenate(packs, axis=1), 'inner', split_axis=0, con...  5.23 us
    unnamed x26, local copies, waits for them, and re-layouts  3.94 us
    dot_general x2, matrix products, unpack_slots(): jnp.einsum('mr,md->rd', placed, arrived.reshape(-1, width), precision=lax...  2.97 us
    dot_general x2, matrix products, pack_slots(): jnp.einsum('nkr,nrd->nkd', picks_f, accum, precision=lax.Precision.HIGHEST)  2.51 us
  transfers between devices with their start and end apart: 2, of which 1 were waited for; matrix products, arithmetic and copies ran while one was open for 12% of the time, Pallas kernels for 0%

commit v1 on v0

--- a/solution.py
+++ b/solution.py
@@ -1,8 +1,11 @@
+import functools
 import math
 
 import jax
 import jax.numpy as jnp
 from jax import lax
+from jax.experimental import pallas as pl
+from jax.experimental.pallas import tpu as pltpu
 from jax.sharding import PartitionSpec as P
 
 step_size = 0.0625
@@ -107,9 +110,333 @@
     return (applied.reshape(rows, cols), resid[None], oresid[None])
 
 
+LANES = 128
+F32 = jnp.float32
+BF16 = jnp.bfloat16
+
+
+def fused_kernel(
+    dims,
+    acts_hbm, cot_hbm, res_hbm, ores_ref, cnt_ref, rank_ref, ocnt_ref, orank_ref,
+    applied_ref, resid_hbm, nores_ref,
+    acts_v, cot_v, res_v, rk_ref, rp_ref, mt_ref, rsend, rrecv, rall_ref, oh_ref,
+    send, recv, xsend, xrecv, ag,
+    in_sem, out_sem, rs_sem, rr_sem, s_sem, r_sem, xs_sem, xr_sem,
+    zs_sem, zr_sem, os_sem, or_sem, ps_sem, pr_sem,
+):
+    n_in, n_out, steps, scale, region, slots, width = dims
+    rows, cols = acts_v.shape[2], cot_v.shape[2]
+    cpr = cols // width
+    rpr = region // cpr
+    halves = region // LANES
+    rpc = LANES // rpr
+    n_z = n_in // 2
+    big = float(region)
+    me = lax.axis_index("inner")
+    pod = lax.axis_index("outer")
+    core = lax.rem(me, 2)
+    z = lax.div(me, 2)
+    partner = me + 1 - 2 * core
+
+    def inner(d):
+        return lax.rem(me + d, n_in)
+
+    def outer(d):
+        return lax.rem(pod + d, n_out)
+
+    def remote(src, dst, ssem, rsem, **device):
+        return pltpu.make_async_remote_copy(
+            src_ref=src, dst_ref=dst, send_sem=ssem, recv_sem=rsem,
+            device_id=device, device_id_type=pl.DeviceIdType.MESH,
+        )
+
+    loads = []
+    for s in range(steps):
+        pair = [
+            pltpu.make_async_copy(acts_hbm.at[s], acts_v.at[s], in_sem.at[2 * s]),
+            pltpu.make_async_copy(cot_hbm.at[s], cot_v.at[s], in_sem.at[2 * s + 1]),
+        ]
+        for copy in pair:
+            copy.start()
+        loads.append(pair)
+        if s == 0:
+            res_load = pltpu.make_async_copy(res_hbm, res_v, in_sem.at[2 * steps])
+            res_load.start()
+
+    barrier = pltpu.get_barrier_semaphore()
+    for d in range(1, n_in):
+        pl.semaphore_signal(barrier, inc=1, device_id={"inner": inner(d)}, device_id_type=pl.DeviceIdType.MESH)
+    for d in range(1, n_out):
+        pl.semaphore_signal(barrier, inc=1, device_id={"outer": outer(d)}, device_id_type=pl.DeviceIdType.MESH)
+
+    rk_ref[...] = jnp.full(rk_ref.shape, big, F32)
+    for s in range(steps):
+        for j in range(n_in):
+            row = rank_ref[s : s + 1, j * region : (j + 1) * region]
+            rk_ref[s * n_in + j : s * n_in + j + 1, :] = jnp.where(
+                row < cnt_ref[s : s + 1, j : j + 1], row.astype(F32), big
+            )
+        row = orank_ref[s : s + 1, :]
+        rk_ref[steps * n_in + s : steps * n_in + s + 1, :] = jnp.where(
+            row < ocnt_ref[0:1, s : s + 1], row.astype(F32), big
+        )
+    old = lax.broadcasted_iota(jnp.int32, (region, region), 0)
+    new = lax.broadcasted_iota(jnp.int32, (region, region), 1)
+    shift = rpr.bit_length() - 1
+    perm = jnp.where(old == (new & (rpr - 1)) * cpr + (new >> shift), 1.0, 0.0).astype(BF16)
+    rp = jnp.dot(rk_ref[...].astype(BF16), perm, preferred_element_type=F32)
+    rp_ref[...] = rp
+    n_rk = rk_ref.shape[0]
+
+    def eye(n):
+        return jnp.where(
+            lax.broadcasted_iota(jnp.int32, (n, LANES), 0) == lax.broadcasted_iota(jnp.int32, (n, LANES), 1), 1.0, 0.0
+        ).astype(BF16)
+
+    def turned(values):
+        return lax.dot_general(
+            values.astype(BF16), eye(values.shape[0]), (((0,), (0,)), ((), ())), preferred_element_type=F32
+        ).astype(BF16)
+
+    def spread(table, index, n):
+        pick = jnp.where(lax.broadcasted_iota(jnp.int32, (LANES, n), 0) == index, 1.0, 0.0).astype(BF16)
+        return jnp.dot(table, pick, preferred_element_type=F32)
+
+    mt_ref[...] = turned(jnp.where(rp < big, 1.0, 0.0))
+    for j in range(n_in):
+        for s in range(steps):
+            for h in range(halves):
+                rsend[j, s * halves + h : s * halves + h + 1, :] = rp_ref[
+                    s * n_in + j : s * n_in + j + 1, h * LANES : (h + 1) * LANES
+                ]
+    pl.semaphore_wait(barrier, n_in - 1 + n_out - 1)
+    sends = []
+    for d in range(1, n_in):
+        copy = remote(rsend.at[inner(d)], rrecv.at[me], rs_sem.at[d], rr_sem.at[me], inner=inner(d))
+        copy.start()
+        sends.append(copy)
+
+    order = []
+    chunks = rows // LANES
+    for a in range((chunks + 1) // 2):
+        order.append(a)
+        if chunks - 1 - a != a:
+            order.append(chunks - 1 - a)
+
+    def packet(s, j):
+        return remote(send.at[s, j], recv.at[s, pl.ds(pl.multiple_of(me * slots, slots), slots)],
+                      s_sem.at[s, j], r_sem.at[s, me], inner=j)
+
+    slot_id = lax.broadcasted_iota(jnp.int32, (slots, region), 0).astype(F32)
+    for s in range(steps):
+        for copy in loads[s]:
+            copy.wait()
+        if s == 0:
+            res_load.wait()
+        for q in order:
+            g = lax.dot_general(
+                acts_v[s, :, q * LANES : (q + 1) * LANES], cot_v[s], (((0,), (0,)), ((), ())),
+                preferred_element_type=F32,
+            ) * scale
+            for half in range(rpc):
+                j = q * rpc + half
+                chosen = spread(mt_ref[...], s * n_in + j, width)
+                picks = jnp.where(rp_ref[s * n_in + j : s * n_in + j + 1, :] == slot_id, 1.0, 0.0).astype(BF16)
+                parts = []
+                for c in range(cpr):
+                    where_at = pl.ds(region * j + c, rpr, stride=cpr)
+                    acc = res_v[where_at, :] + g[half * rpr : (half + 1) * rpr, c * width : (c + 1) * width]
+                    res_v[where_at, :] = jnp.where(chosen[c * rpr : (c + 1) * rpr] > 0.5, 0.0, acc)
+                    parts.append(acc)
+                packed = jnp.dot(picks, jnp.concatenate(parts, axis=0).astype(BF16), preferred_element_type=F32)
+                send[s, j] = packed.astype(BF16)
+
+                @pl.when(me != j)
+                def _():
+                    packet(s, j).start()
+
+    resid_out = pltpu.make_async_copy(res_v, resid_hbm, out_sem)
+    resid_out.start()
+
+    rrecv[me] = rsend[me]
+    for d in range(1, n_in):
+        i = inner(d)
+        remote(rrecv.at[i], rrecv.at[i], rs_sem.at[d], rr_sem.at[i], inner=i).wait_recv()
+    for i in range(n_in):
+        for s in range(steps):
+            for h in range(halves):
+                rall_ref[s * n_in + i : s * n_in + i + 1, h * LANES : (h + 1) * LANES] = rrecv[
+                    i, s * halves + h : s * halves + h + 1, :
+                ]
+    rt = turned(rall_ref[...])
+    lane_id = lax.broadcasted_iota(jnp.int32, (region, slots), 1).astype(F32)
+    for s in range(steps):
+        for i in range(n_in):
+            oh_ref[s, :, i * slots : (i + 1) * slots] = jnp.where(
+                spread(rt, s * n_in + i, slots) == lane_id, 1.0, 0.0
+            ).astype(BF16)
+
+    oresid = jnp.concatenate([ores_ref[pl.ds(c, rpr, stride=cpr), :] for c in range(cpr)], axis=0)
+    for s in range(steps):
+        recv[s, pl.ds(pl.multiple_of(me * slots, slots), slots)] = send[s, me]
+        for d in range(1, n_in):
+            i = inner(d)
+            spot = recv.at[s, pl.ds(pl.multiple_of(i * slots, slots), slots)]
+            remote(spot, spot, s_sem.at[s, 0], r_sem.at[s, i], inner=i).wait_recv()
+        oacc = jnp.dot(oh_ref[s], recv[s], preferred_element_type=F32) + oresid
+        passed = spread(mt_ref[...], steps * n_in + s, width) > 0.5
+        outgoing = jnp.where(passed, oacc, 0.0).astype(BF16)
+        oresid = jnp.where(passed, 0.0, oacc)
+        for c in range(n_out):
+            xsend[s, c] = outgoing[c * rpr : (c + 1) * rpr]
+        for d in range(1, n_out):
+            copy = remote(xsend.at[s, outer(d)], xrecv.at[s, pod], xs_sem.at[s, d], xr_sem.at[s, pod], outer=outer(d))
+            copy.start()
+            sends.append(copy)
+    for c in range(cpr):
+        nores_ref[pl.ds(c, rpr, stride=cpr), :] = oresid[c * rpr : (c + 1) * rpr]
+
+    total = jnp.zeros((rpr, width), F32)
+    for s in range(steps):
+        cross = xsend[s, pod].astype(F32)
+        for d in range(1, n_out):
+            i = outer(d)
+            remote(xrecv.at[s, i], xrecv.at[s, i], xs_sem.at[s, d], xr_sem.at[s, i], outer=i).wait_recv()
+            cross = cross + xrecv[s, i].astype(F32)
+        total = total + cross.astype(BF16).astype(F32)
+    ag[core, pod, z] = (-step_size * total).astype(BF16)
+
+    def forward(zz, slot):
+        piece = ag.at[core, pod, zz]
+        for d in range(1, n_out):
+            copy = remote(piece, piece, os_sem.at[slot, d], or_sem.at[pod, zz], outer=outer(d))
+            copy.start()
+            sends.append(copy)
+
+    def hand_over(q, slot):
+        piece = ag.at[core, q]
+        copy = remote(piece, piece, ps_sem.at[slot], pr_sem.at[q], inner=partner)
+        copy.start()
+        sends.append(copy)
+
+    own = ag.at[core, pod, z]
+    for d in range(1, n_z):
+        copy = remote(own, own, zs_sem.at[d], zr_sem.at[z], inner=inner(2 * d))
+        copy.start()
+        sends.append(copy)
+    forward(z, 0)
+    for d in range(1, n_z):
+        zz = lax.rem(z + d, n_z)
+        piece = ag.at[core, pod, zz]
+        remote(piece, piece, zs_sem.at[d], zr_sem.at[zz], inner=inner(2 * d)).wait_recv()
+        forward(zz, d)
+    hand_over(pod, 0)
+    for d in range(1, n_out):
+        q = outer(d)
+        for zz in range(n_z):
+            piece = ag.at[core, q, zz]
+            remote(piece, piece, os_sem.at[0, d], or_sem.at[q, zz], outer=q).wait_recv()
+        hand_over(q, d)
+    for d in range(n_out):
+        q = outer(d)
+        piece = ag.at[1 - core, q]
+        remote(piece, piece, ps_sem.at[d], pr_sem.at[q], inner=partner).wait_recv()
+    for zz in range(n_z):
+        for k in range(2):
+            j = zz * 2 + k
+            for q in range(n_out):
+                applied_ref[j * rpr : (j + 1) * rpr, q * width : (q + 1) * width] = ag[k, q, zz]
+
+    for copy in sends:
+        copy.wait_send()
+    for s in range(steps):
+        for j in range(n_in):
+
+            @pl.when(me != j)
+            def _():
+                packet(s, j).wait_send()
+
+    resid_out.wait()
+
+
+def fits(owners, pods, steps, rows, cols, blocks, width, region, slots):
+    if width != LANES or slots % LANES or region % LANES or region > 256 or cols % width:
+        return False
+    cpr = cols // width
+    rpr = region // cpr
+    return (
+        cpr == pods and cpr * rpr == region and rpr % 16 == 0 and LANES % rpr == 0 and rpr & (rpr - 1) == 0
+        and rows % LANES == 0 and owners >= 4 and owners % 2 == 0
+        and rpr * owners == rows and steps * (owners + 1) <= LANES and steps * (region // LANES) <= 8
+    )
+
+
+def per_device_fused(acts, cotangent, residual, owner_residual, in_count, in_rank, out_count, out_rank):
+    n_in = lax.axis_size("inner")
+    n_out = lax.axis_size("outer")
+    steps, tokens, rows = acts.shape[1:]
+    cols = cotangent.shape[3]
+    blocks, width = residual.shape[1:]
+    region = blocks // n_in
+    slots = max(1, region // 2)
+    if not fits(n_in, n_out, steps, rows, cols, blocks, width, region, slots):
+        return per_device(acts, cotangent, residual, owner_residual, in_count, in_rank, out_count, out_rank)
+    scale = 1.0 / math.sqrt(tokens * n_in)
+    rpr = region // n_out
+    n_z = n_in // 2
+    n_rk = -(-steps * (n_in + 1) // 16) * 16
+    n_ra = -(-steps * n_in // 16) * 16
+    vmem = pl.BlockSpec(memory_space=pltpu.VMEM)
+    anywhere = pl.BlockSpec(memory_space=pl.ANY)
+    dma = pltpu.SemaphoreType.DMA
+    applied, resid, oresid = pl.pallas_call(
+        functools.partial(fused_kernel, (n_in, n_out, steps, scale, region, slots, width)),
+        out_shape=(
+            jax.ShapeDtypeStruct((rows, cols), BF16),
+            jax.ShapeDtypeStruct((blocks, width), F32),
+            jax.ShapeDtypeStruct((region, width), F32),
+        ),
+        in_specs=[anywhere, anywhere, anywhere, vmem, vmem, vmem, vmem, vmem],
+        out_specs=(vmem, anywhere, vmem),
+        scratch_shapes=[
+            pltpu.VMEM((steps, tokens, rows), BF16),
+            pltpu.VMEM((steps, tokens, cols), BF16),
+            pltpu.VMEM((blocks, width), F32),
+            pltpu.VMEM((n_rk, region), F32),
+            pltpu.VMEM((n_rk, region), F32),
+            pltpu.VMEM((region, LANES), BF16),
+            pltpu.VMEM((n_in, 8, LANES), F32),
+            pltpu.VMEM((n_in, 8, LANES), F32),
+            pltpu.VMEM((n_ra, region), F32),
+            pltpu.VMEM((steps, region, n_in * slots), BF16),
+            pltpu.VMEM((steps, n_in, slots, width), BF16),
+            pltpu.VMEM((steps, n_in * slots, width), BF16),
+            pltpu.VMEM((steps, n_out, rpr, width), BF16),
+            pltpu.VMEM((steps, n_out, rpr, width), BF16),
+            pltpu.VMEM((2, n_out, n_z, rpr, width), BF16),
+            dma((2 * steps + 1,)),
+            dma,
+            dma((n_in,)),
+            dma((n_in,)),
+            dma((steps, n_in)),
+            dma((steps, n_in)),
+            dma((steps, n_out)),
+            dma((steps, n_out)),
+            dma((n_z,)),
+            dma((n_z,)),
+            dma((n_z, n_out)),
+            dma((n_out, n_z)),
+            dma((n_out,)),
+            dma((n_out,)),
+        ],
+        compiler_params=pltpu.CompilerParams(collective_id=0, has_side_effects=True),
+    )(acts[0], cotangent[0], residual[0], owner_residual[0], in_count[0], in_rank[0], out_count, out_rank[0])
+    return applied, resid[None], oresid[None]
+
+
 def solution(mesh):
     return jax.shard_map(
-        per_device,
+        per_device_fused,
         mesh=mesh,
         in_specs=(
             P(("outer", "inner"), None, None, None),

time: 108 us -> 38 us (0.35)
  blocking collectives: 51.4 us -> 0 us
  Pallas kernels: 0 us -> 33.6 us
  waiting for transfers between devices: 18.6 us -> 0 us
  starting transfers between devices: 11.6 us -> 0 us
  matrix products: 8.8 us -> 0 us
  local copies, waits for them, and re-layouts: 10.9 us -> 3.64 us
  other arithmetic: 5.26 us -> 0 us
    all_gather x2 -> x0, blocking collectives: 34.8 us -> none  [per_device(): deltas.append(lax.all_gather(delta, 'inner', axis=0, tiled=True))]
    pallas_call x0 -> x1, Pallas kernels: none -> 33.6 us  [per_device_fused(): pl.pallas_call(functools.partial(fused_kernel, (n_in, n_out, steps, scale...]
    all_to_all x2 -> x0, waiting for transfers between devices: 18.6 us -> none  [the longest x1 18.6 us: per_device(): lax.all_to_all(jnp.concatenate(packs, axis=1), 'inner', split_axis=0, con...]
    psum x1 -> x0, blocking collectives: 16.5 us -> none  [per_device(): summed = lax.psum(jnp.stack(outgoings), 'outer')]
    all_to_all x2 -> x0, starting transfers between devices: 11.6 us -> none  [the longest x1 6.37 us: per_device(): lax.all_to_all(jnp.concatenate(spots_all, axis=1), 'inner', split_axis=0,...]
    dot_general x8 -> x0, matrix products: 8.8 us -> none  [the longest x2 2.97 us: unpack_slots(): jnp.einsum('mr,md->rd', placed, arrived.reshape(-1, width), precision=lax...]
    reshape x5 -> x0, local copies, waits for them, and re-layouts: 3.58 us -> none  [the longest x4 2.47 us: select_blocks(): accum = (resid + grad.reshape(blocks, width)).reshape(owners, region, width)]
    slice x4 -> x0, local copies, waits for them, and re-layouts: 2.73 us -> none  [the longest x1 1.29 us: per_device(): arrived[:, step * slots:(step + 1) * slots]]
  transfers between devices with their start and end apart: 2 -> 0, of which waited for: 1 -> 0; matrix products, arithmetic and copies ran while one was open for 12% -> 0% of each run, Pallas kernels for 0% -> 0%
where the time goes in v1:
time: 38 us; the launch traced here: 37.8 us
  Pallas kernels  33.6 us (88%)
  local copies, waits for them, and re-layouts  3.64 us (10%)
  between operations  0.65 us (2%)
    pallas_call x1, Pallas kernels, per_device_fused(): pl.pallas_call(functools.partial(fused_kernel, (n_in, n_out, steps, scale...  33.6 us
    unnamed x7, local copies, waits for them, and re-layouts  3.64 us

profile of v1, /device:TPU:1, one launch (start us, length us, event | category | flops | bytes accessed | tf_op | source)
XLA Modules:
  0.0 37.8 jit_solution(17518291209968577514)
XLA Ops:
  0.6 33.6 %shard_map.103 = (bf16[512,512]{1,0:T(8,128)(2,1)}, f32[2048,128]{1,0:T(8,128)}, f32[256,128]{1,0:T(8,128)}) custom-call(bf16[2,512,512]{2,1,0:T(8,128)(2,1)} %bitcast.9, bf16[2,512,512]{2,1,0:T(8,128)(2,1)} %bitcast.10, f32[2048,128]{1,0:T(8,128)} %bitcast.11, f32[256,128]{1,0:T(8,128)} %bitcast.13, s32[2,8]{1,0:T(2,128)} %bitcast.17, s32[2,2048]{1,0:T(2,128)} %bitcast.15, ...), custom_call_target="tpu_custom_call" | custom-call | tf_op jit(solution)/shard_map/pallas_call | solution.py:392
  34.2 0.0 copy-start
  34.2 2.0 %copy.14 = bf16[512,512]{1,0:T(8,128)(2,1)} copy(bf16[512,512]{1,0:T(8,128)(2,1)} %get-tuple-element.12) | data formatting | bytes 1048576
  36.2 0.0 copy-done
  36.2 0.0 copy-start.1
  36.2 1.0 %copy.15 = f32[1,2048,128]{2,1,0:T(8,128)} copy(f32[1,2048,128]{2,1,0:T(8,128)S(1)} %bitcast.12) | data formatting | bytes 2097152
  37.1 0.1 copy-done.1
  37.2 0.7 %copy.16 = f32[1,256,128]{2,1,0:T(8,128)} copy(f32[1,256,128]{2,1,0:T(8,128)S(1)} %bitcast.14) | data formatting | bytes 262144
Async XLA Ops:
  34.2 2.0 %copy-start = (f32[2048,128]{1,0:T(8,128)S(1)}, f32[2048,128]{1,0:T(8,128)}, u32[]{:S(2)}) copy-start(f32[2048,128]{1,0:T(8,128)} %get-tuple-element.7) | copy-start | bytes 3145732
  36.2 1.0 %copy-start.1 = (f32[256,128]{1,0:T(8,128)S(1)}, f32[256,128]{1,0:T(8,128)}, u32[]{:S(2)}) copy-start(f32[256,128]{1,0:T(8,128)} %get-tuple-element.8) | copy-start | bytes 393220

commit v2 on v1

--- a/solution.py
+++ b/solution.py
@@ -118,10 +118,10 @@
 def fused_kernel(
     dims,
     acts_hbm, cot_hbm, res_hbm, ores_ref, cnt_ref, rank_ref, ocnt_ref, orank_ref,
-    applied_ref, resid_hbm, nores_ref,
+    applied_ref, resid_ref, nores_ref,
     acts_v, cot_v, res_v, rk_ref, rp_ref, mt_ref, rsend, rrecv, rall_ref, oh_ref,
     send, recv, xsend, xrecv, ag,
-    in_sem, out_sem, rs_sem, rr_sem, s_sem, r_sem, xs_sem, xr_sem,
+    in_sem, rs_sem, rr_sem, s_sem, r_sem, xs_sem, xr_sem,
     zs_sem, zr_sem, os_sem, or_sem, ps_sem, pr_sem,
 ):
     n_in, n_out, steps, scale, region, slots, width = dims
@@ -246,7 +246,8 @@
                 for c in range(cpr):
                     where_at = pl.ds(region * j + c, rpr, stride=cpr)
                     acc = res_v[where_at, :] + g[half * rpr : (half + 1) * rpr, c * width : (c + 1) * width]
-                    res_v[where_at, :] = jnp.where(chosen[c * rpr : (c + 1) * rpr] > 0.5, 0.0, acc)
+                    kept = jnp.where(chosen[c * rpr : (c + 1) * rpr] > 0.5, 0.0, acc)
+                    (resid_ref if s == steps - 1 else res_v)[where_at, :] = kept
                     parts.append(acc)
                 packed = jnp.dot(picks, jnp.concatenate(parts, axis=0).astype(BF16), preferred_element_type=F32)
                 send[s, j] = packed.astype(BF16)
@@ -255,8 +256,6 @@
                 def _():
                     packet(s, j).start()
 
-    resid_out = pltpu.make_async_copy(res_v, resid_hbm, out_sem)
-    resid_out.start()
 
     rrecv[me] = rsend[me]
     for d in range(1, n_in):
@@ -356,7 +355,26 @@
             def _():
                 packet(s, j).wait_send()
 
-    resid_out.wait()
+
+def hand_out(*arrays):
+    n = len(arrays)
+
+    def kernel(*refs):
+        sems = refs[2 * n]
+        copies = [pltpu.make_async_copy(refs[k], refs[n + k], sems.at[k]) for k in range(n)]
+        for copy in copies:
+            copy.start()
+        for copy in copies:
+            copy.wait()
+
+    return pl.pallas_call(
+        kernel,
+        out_shape=tuple(jax.ShapeDtypeStruct(a.shape, a.dtype) for a in arrays),
+        in_specs=[pl.BlockSpec(memory_space=pltpu.VMEM)] * n,
+        out_specs=tuple([pl.BlockSpec(memory_space=pltpu.HBM)] * n),
+        scratch_shapes=[pltpu.SemaphoreType.DMA((n,))],
+        compiler_params=pltpu.CompilerParams(vmem_limit_bytes=4 << 20),
+    )(*arrays)
 
 
 def fits(owners, pods, steps, rows, cols, blocks, width, region, slots):
@@ -387,7 +405,7 @@
     n_rk = -(-steps * (n_in + 1) // 16) * 16
     n_ra = -(-steps * n_in // 16) * 16
     vmem = pl.BlockSpec(memory_space=pltpu.VMEM)
-    anywhere = pl.BlockSpec(memory_space=pl.ANY)
+    anywhere = pl.BlockSpec(memory_space=pltpu.HBM)
     dma = pltpu.SemaphoreType.DMA
     applied, resid, oresid = pl.pallas_call(
         functools.partial(fused_kernel, (n_in, n_out, steps, scale, region, slots, width)),
@@ -397,7 +415,7 @@
             jax.ShapeDtypeStruct((region, width), F32),
         ),
         in_specs=[anywhere, anywhere, anywhere, vmem, vmem, vmem, vmem, vmem],
-        out_specs=(vmem, anywhere, vmem),
+        out_specs=(vmem, vmem, vmem),
         scratch_shapes=[
             pltpu.VMEM((steps, tokens, rows), BF16),
             pltpu.VMEM((steps, tokens, cols), BF16),
@@ -415,7 +433,6 @@
             pltpu.VMEM((steps, n_out, rpr, width), BF16),
             pltpu.VMEM((2, n_out, n_z, rpr, width), BF16),
             dma((2 * steps + 1,)),
-            dma,
             dma((n_in,)),
             dma((n_in,)),
             dma((steps, n_in)),
@@ -429,8 +446,9 @@
             dma((n_out,)),
             dma((n_out,)),
         ],
-        compiler_params=pltpu.CompilerParams(collective_id=0, has_side_effects=True),
+        compiler_params=pltpu.CompilerParams(collective_id=0, has_side_effects=True, vmem_limit_bytes=24 << 20),
     )(acts[0], cotangent[0], residual[0], owner_residual[0], in_count[0], in_rank[0], out_count, out_rank[0])
+    applied, resid, oresid = hand_out(applied, resid, oresid)
     return applied, resid[None], oresid[None]
 
 

time: 38 us -> 40.1 us (1.055)
  local copies, waits for them, and re-layouts: 3.64 us -> 5.97 us
  Pallas kernels: 33.6 us -> 33.1 us
    unnamed x7 -> x16, local copies, waits for them, and re-layouts: 3.64 us -> 5.97 us
    pallas_call x1, Pallas kernels: 33.6 us -> 31.9 us  [per_device_fused(): pl.pallas_call(functools.partial(fused_kernel, (n_in, n_out, steps, scale...]
    pallas_call x0 -> x1, Pallas kernels: none -> 1.2 us  [hand_out(): pl.pallas_call(kernel, out_shape=tuple((jax.ShapeDtypeStruct(a.shape, a.d...]
where the time goes in v2:
time: 40.1 us; the launch traced here: 39.8 us
  Pallas kernels  33.1 us (83%)
  local copies, waits for them, and re-layouts  5.97 us (15%)
  between operations  0.67 us (2%)
    pallas_call x1, Pallas kernels, per_device_fused(): pl.pallas_call(functools.partial(fused_kernel, (n_in, n_out, steps, scale...  31.9 us
    unnamed x16, local copies, waits for them, and re-layouts  5.97 us
    pallas_call x1, Pallas kernels, hand_out(): pl.pallas_call(kernel, out_shape=tuple((jax.ShapeDtypeStruct(a.shape, a.d...  1.2 us

profile of v2, /device:TPU:1, one launch (start us, length us, event | category | flops | bytes accessed | tf_op | source)
XLA Modules:
  0.0 39.8 jit_solution(10113461613772704847)
XLA Ops:
  0.6 0.0 copy-start.5
  0.6 0.0 copy-start.6
  0.7 0.0 copy-start.7
  0.7 0.7 %copy-done.5 = s32[1,2,256]{2,1,0:T(2,128)S(1)} copy-done((s32[1,2,256]{2,1,0:T(2,128)S(1)}, s32[1,2,256]{2,1,0:T(2,128)}, u32[]{:S(2)}) %copy-start.5) | copy-done | bytes 2072
  1.3 0.0 copy-done.6
  1.3 0.0 copy-done.7
  1.3 0.0 copy-start
  1.3 1.2 %copy-done = bf16[1,2,512,512]{3,2,1,0:T(8,128)(2,1)S(1)} copy-done((bf16[1,2,512,512]{3,2,1,0:T(8,128)(2,1)S(1)}, bf16[1,2,512,512]{3,2,1,0:T(8,128)(2,1)}, u32[]{:S(2)}) %copy-start) | copy-done | bytes 1048600
  2.6 0.0 copy-start.1
  2.6 1.2 %copy-done.1 = bf16[1,2,512,512]{3,2,1,0:T(8,128)(2,1)S(1)} copy-done((bf16[1,2,512,512]{3,2,1,0:T(8,128)(2,1)S(1)}, bf16[1,2,512,512]{3,2,1,0:T(8,128)(2,1)}, u32[]{:S(2)}) %copy-start.1) | copy-done | bytes 1048600
  3.8 0.0 copy-start.2
  3.8 1.2 %copy-done.2 = f32[1,2048,128]{2,1,0:T(8,128)S(1)} copy-done((f32[1,2048,128]{2,1,0:T(8,128)S(1)}, f32[1,2048,128]{2,1,0:T(8,128)}, u32[]{:S(2)}) %copy-start.2) | copy-done | bytes 1048600
  5.0 0.0 copy-start.3
  5.0 0.9 %copy-done.3 = f32[1,256,128]{2,1,0:T(8,128)S(1)} copy-done((f32[1,256,128]{2,1,0:T(8,128)S(1)}, f32[1,256,128]{2,1,0:T(8,128)}, u32[]{:S(2)}) %copy-start.3) | copy-done | bytes 131096
  5.9 0.0 copy-start.4
  5.9 0.7 %copy-done.4 = s32[1,2,2048]{2,1,0:T(2,128)S(1)} copy-done((s32[1,2,2048]{2,1,0:T(2,128)S(1)}, s32[1,2,2048]{2,1,0:T(2,128)}, u32[]{:S(2)}) %copy-start.4) | copy-done | bytes 16408
  6.6 31.9 %shard_map.103 = (bf16[512,512]{1,0:T(8,128)(2,1)S(1)}, f32[2048,128]{1,0:T(8,128)S(1)}, f32[256,128]{1,0:T(8,128)S(1)}) custom-call(bf16[2,512,512]{2,1,0:T(8,128)(2,1)S(1)} %bitcast.9, bf16[2,512,512]{2,1,0:T(8,128)(2,1)S(1)} %bitcast.10, f32[2048,128]{1,0:T(8,128)S(1)} %bitcast.11, f32[256,128]{1,0:T(8,128)S(1)} %bitcast.12, s32[2,8]{1,0:T(2,128)S(1)} %bitcast.15, ...), custom_call_target="tpu_custom_call" | custom-call | tf_op jit(solution)/shard_map/pallas_call | solution.py:410
  38.6 1.2 %shard_map.104 = (bf16[512,512]{1,0:T(8,128)(2,1)}, f32[2048,128]{1,0:T(8,128)}, f32[256,128]{1,0:T(8,128)}) custom-call(bf16[512,512]{1,0:T(8,128)(2,1)S(1)} %get-tuple-element.9.refs_0_, f32[2048,128]{1,0:T(8,128)S(1)} %get-tuple-element.10.refs_1_, f32[256,128]{1,0:T(8,128)S(1)} %get-tuple-element.11.refs_2_), custom_call_target="tpu_custom_call" | custom-call | tf_op jit(solution)/shard_map/pallas_call | solution.py:370
Async XLA Ops:
  0.6 0.7 %copy-start.5 = (s32[1,2,256]{2,1,0:T(2,128)S(1)}, s32[1,2,256]{2,1,0:T(2,128)}, u32[]{:S(2)}) copy-start(s32[1,2,256]{2,1,0:T(2,128)} %param.15) | copy-start | bytes 6148
  0.6 0.7 %copy-start.6 = (s32[1,2,8]{2,1,0:T(2,128)S(1)}, s32[1,2,8]{2,1,0:T(2,128)}, u32[]{:S(2)}) copy-start(s32[1,2,8]{2,1,0:T(2,128)} %param.12) | copy-start | bytes 196
  0.7 0.7 %copy-start.7 = (s32[1,2]{1,0:T(1,128)S(1)}, s32[1,2]{1,0:T(1,128)}, u32[]{:S(2)}) copy-start(s32[1,2]{1,0:T(1,128)} %ocnt_ref.1) | copy-start | bytes 28
  1.3 1.2 %copy-start = (bf16[1,2,512,512]{3,2,1,0:T(8,128)(2,1)S(1)}, bf16[1,2,512,512]{3,2,1,0:T(8,128)(2,1)}, u32[]{:S(2)}) copy-start(bf16[1,2,512,512]{3,2,1,0:T(8,128)(2,1)} %param.8) | copy-start | bytes 3145732
  2.6 1.2 %copy-start.1 = (bf16[1,2,512,512]{3,2,1,0:T(8,128)(2,1)S(1)}, bf16[1,2,512,512]{3,2,1,0:T(8,128)(2,1)}, u32[]{:S(2)}) copy-start(bf16[1,2,512,512]{3,2,1,0:T(8,128)(2,1)} %param.9) | copy-start | bytes 3145732
  3.8 1.2 %copy-start.2 = (f32[1,2048,128]{2,1,0:T(8,128)S(1)}, f32[1,2048,128]{2,1,0:T(8,128)}, u32[]{:S(2)}) copy-start(f32[1,2048,128]{2,1,0:T(8,128)} %param.10) | copy-start | bytes 3145732
  5.0 0.9 %copy-start.3 = (f32[1,256,128]{2,1,0:T(8,128)S(1)}, f32[1,256,128]{2,1,0:T(8,128)}, u32[]{:S(2)}) copy-start(f32[1,256,128]{2,1,0:T(8,128)} %param.11) | copy-start | bytes 393220
  5.9 0.7 %copy-start.4 = (s32[1,2,2048]{2,1,0:T(2,128)S(1)}, s32[1,2,2048]{2,1,0:T(2,128)}, u32[]{:S(2)}) copy-start(s32[1,2,2048]{2,1,0:T(2,128)} %param.13) | copy-start | bytes 49156

commit v3 on v2

--- a/solution.py
+++ b/solution.py
@@ -117,8 +117,9 @@
 
 def fused_kernel(
     dims,
-    acts_hbm, cot_hbm, res_hbm, ores_ref, cnt_ref, rank_ref, ocnt_ref, orank_ref,
+    acts_hbm, cot_hbm, res_hbm, ores_hbm, cnt_hbm, rank_hbm, ocnt_hbm, orank_hbm,
     applied_ref, resid_ref, nores_ref,
+    ores_ref, cnt_ref, rank_ref, ocnt_ref, orank_ref, small_sem,
     acts_v, cot_v, res_v, rk_ref, rp_ref, mt_ref, rsend, rrecv, rall_ref, oh_ref,
     send, recv, xsend, xrecv, ag,
     in_sem, rs_sem, rr_sem, s_sem, r_sem, xs_sem, xr_sem,
@@ -150,6 +151,14 @@
             device_id=device, device_id_type=pl.DeviceIdType.MESH,
         )
 
+    small = [
+        pltpu.make_async_copy(src, dst, small_sem.at[k])
+        for k, (src, dst) in enumerate(
+            ((rank_hbm, rank_ref), (cnt_hbm, cnt_ref), (orank_hbm, orank_ref), (ocnt_hbm, ocnt_ref), (ores_hbm, ores_ref))
+        )
+    ]
+    for copy in small:
+        copy.start()
     loads = []
     for s in range(steps):
         pair = [
@@ -170,6 +179,8 @@
         pl.semaphore_signal(barrier, inc=1, device_id={"outer": outer(d)}, device_id_type=pl.DeviceIdType.MESH)
 
     rk_ref[...] = jnp.full(rk_ref.shape, big, F32)
+    for copy in small:
+        copy.wait()
     for s in range(steps):
         for j in range(n_in):
             row = rank_ref[s : s + 1, j * region : (j + 1) * region]
@@ -414,9 +425,15 @@
             jax.ShapeDtypeStruct((blocks, width), F32),
             jax.ShapeDtypeStruct((region, width), F32),
         ),
-        in_specs=[anywhere, anywhere, anywhere, vmem, vmem, vmem, vmem, vmem],
+        in_specs=[anywhere] * 8,
         out_specs=(vmem, vmem, vmem),
         scratch_shapes=[
+            pltpu.VMEM((region, width), F32),
+            pltpu.VMEM((steps, n_in), jnp.int32),
+            pltpu.VMEM((steps, blocks), jnp.int32),
+            pltpu.VMEM((1, steps), jnp.int32),
+            pltpu.VMEM((steps, region), jnp.int32),
+            dma((5,)),
             pltpu.VMEM((steps, tokens, rows), BF16),
             pltpu.VMEM((steps, tokens, cols), BF16),
             pltpu.VMEM((blocks, width), F32),
@@ -446,8 +463,13 @@
             dma((n_out,)),
             dma((n_out,)),
         ],
-        compiler_params=pltpu.CompilerParams(collective_id=0, has_side_effects=True, vmem_limit_bytes=24 << 20),
-    )(acts[0], cotangent[0], residual[0], owner_residual[0], in_count[0], in_rank[0], out_count, out_rank[0])
+        compiler_params=pltpu.CompilerParams(collective_id=0, has_side_effects=True, vmem_limit_bytes=48 << 20),
+    )(*(
+        pltpu.with_memory_space_constraint(a, pltpu.HBM)
+        for a in (
+            acts[0], cotangent[0], residual[0], owner_residual[0], in_count[0], in_rank[0], out_count, out_rank[0]
+        )
+    ))
     applied, resid, oresid = hand_out(applied, resid, oresid)
     return applied, resid[None], oresid[None]
 

time: 40.1 us -> 33.9 us (0.85)
  local copies, waits for them, and re-layouts: 5.97 us -> 0 us
    unnamed x16 -> x0, local copies, waits for them, and re-layouts: 5.97 us -> none
where the time goes in v3:
time: 33.9 us; the launch traced here: 33.7 us
  Pallas kernels  33 us (97%)
  between operations  0.64 us (2%)
    pallas_call x1, Pallas kernels, per_device_fused(): pl.pallas_call(functools.partial(fused_kernel, (n_in, n_out, steps, scale...  31.8 us
    pallas_call x1, Pallas kernels, hand_out(): pl.pallas_call(kernel, out_shape=tuple((jax.ShapeDtypeStruct(a.shape, a.d...  1.2 us

profile of v3, /device:TPU:1, one launch (start us, length us, event | category | flops | bytes accessed | tf_op | source)
XLA Modules:
  0.0 33.7 jit_solution(12429981556202038092)
XLA Ops:
  0.6 31.8 %shard_map.103 = (bf16[512,512]{1,0:T(8,128)(2,1)S(1)}, f32[2048,128]{1,0:T(8,128)S(1)}, f32[256,128]{1,0:T(8,128)S(1)}) custom-call(bf16[2,512,512]{2,1,0:T(8,128)(2,1)} %bitcast.9, bf16[2,512,512]{2,1,0:T(8,128)(2,1)} %bitcast.10, f32[2048,128]{1,0:T(8,128)} %bitcast.11, f32[256,128]{1,0:T(8,128)} %bitcast.12, s32[2,8]{1,0:T(2,128)} %bitcast.15, ...), custom_call_target="tpu_custom_call" | custom-call | tf_op jit(solution)/shard_map/pallas_call | solution.py:421
  32.5 1.2 %shard_map.104 = (bf16[512,512]{1,0:T(8,128)(2,1)}, f32[2048,128]{1,0:T(8,128)}, f32[256,128]{1,0:T(8,128)}) custom-call(bf16[512,512]{1,0:T(8,128)(2,1)S(1)} %get-tuple-element.9.refs_0_, f32[2048,128]{1,0:T(8,128)S(1)} %get-tuple-element.10.refs_1_, f32[256,128]{1,0:T(8,128)S(1)} %get-tuple-element.11.refs_2_), custom_call_target="tpu_custom_call" | custom-call | tf_op jit(solution)/shard_map/pallas_call | solution.py:381
